TPU v7x, 512 devices: a 4x2x32 block of a 4x8x32 slice. The times are simulated.
512 devices in a mesh: groups: 2 (over y), pix: 32 (over z), sub: 4 (over x), rep: 2 (over core).
Axes of the slice: x: 4, y: 2, z: 32, core: 2. Of those that a mesh axis runs over, the one named last changes fastest.
The devices are a block of a 4x8x32 slice.
Arguments:
- gaia_pos: float32 [2, 65536], P(None, ('groups', 'pix', 'sub', 'rep')), parts along dimension 1, may hold values from 0 to 1
- gaia_shape: float32 [2, 65536], P(None, ('groups', 'pix', 'sub', 'rep')), parts along dimension 1, may hold values from 0.15 to 0.6
- gaia_corr: float32 [65536], P(('groups', 'pix', 'sub', 'rep')), parts along dimension 0, may hold values from -0.8 to 0.8
- gaia_dest: int32 [65536, 1], P(('groups', 'pix', 'sub', 'rep')), parts along dimension 0, may hold values from 0 to 127; in each aligned block of 128 rows (0 to 127, 128 to 255, ...) at most 2 rows name the same one
- gaia_cell: int32 [65536], P(('groups', 'pix', 'sub', 'rep')), parts along dimension 0, may hold values from 0 to 127
- wise_pos: float32 [2, 65536], P(None, ('groups', 'pix', 'sub', 'rep')), parts along dimension 1, may hold values from 0 to 1
- wise_shape: float32 [2, 65536], P(None, ('groups', 'pix', 'sub', 'rep')), parts along dimension 1, may hold values from 0.15 to 0.6
- wise_corr: float32 [65536], P(('groups', 'pix', 'sub', 'rep')), parts along dimension 0, may hold values from -0.8 to 0.8
- wise_dest: int32 [65536, 1], P(('groups', 'pix', 'sub', 'rep')), parts along dimension 0, may hold values from 0 to 127; in each aligned block of 128 rows (0 to 127, 128 to 255, ...) at most 2 rows name the same one
- wise_cell: int32 [65536], P(('groups', 'pix', 'sub', 'rep')), parts along dimension 0, may hold values from 0 to 127
Outputs:
- gaia_like: float32 [65536], P(('groups', 'pix', 'sub', 'rep')), parts along dimension 0
- gaia_offset: float32 [2, 65536], P(None, ('groups', 'pix', 'sub', 'rep')), parts along dimension 1
- wise_like: float32 [65536], P(('groups', 'pix', 'sub', 'rep')), parts along dimension 0
There are 2 independent parts, one for each index of `groups`. A program takes and returns all parts, laid end to end along the dimension named above; each array names one. Nothing has to cross between parts.
Inputs may be any that keep to these rules, and one draw needn't show every extreme that they name: `gaia_dest`: among the 128 sources of one device no target appears more than 2 times, and some target appears exactly 2 times; the owner of a source is dest // 4. `wise_dest`: among the 128 sources of one device no target appears more than 2 times, and some target appears exactly 2 times; the owner of a source is dest // 4. `gaia_cell`: pixel row inside the band is cell // 64, column cell % 64. `wise_cell`: pixel row inside the band is cell // 64, column cell % 64.
All inputs are finite; a program needn't handle non-finite values.
Results may differ from a plain program's by a relative error of at most 0.0003.
Values sent between devices are 32-bit elements; how exact they have to be, the bound alone decides.
No kernel may reach another device: no remote copies, remote signals or barrier semaphores. Data moves between devices by JAX's collectives and lax.ppermute only.
A program may use at most 64 MiB of HBM per device.

v0:
```python
import jax
import jax.numpy as jnp
from jax import lax
from jax.sharding import PartitionSpec as P

SRC_DEV = 128
BAND = 2
NCOL = 64
empty_gaia = -1000.0
empty_wise = -3000.0
row_offset = 4.0
inv_two_pi = 0.15915494309189535


def side_by_side(arrays, axis, split_dim, concat_dim, along):
    ends, at = ([], 0)
    for a in arrays[:-1]:
        at += a.shape[along]
        ends.append(at)
    both = jnp.concatenate(arrays, axis=along)
    return tuple(
        jnp.split(
            lax.all_to_all(both, axis, split_axis=split_dim, concat_axis=concat_dim, tiled=True),
            ends,
            axis=along,
        )
    )


def with_halo(x, sides, width):
    for axis, dim in sides:
        size, length = (lax.axis_size(axis), x.shape[dim])
        up = [(i, (i + 1) % size) for i in range(size - 1)]
        down = [(j, i) for i, j in up]
        last = lax.slice_in_dim(x, length - width, length, axis=dim)
        leading = lax.slice_in_dim(x, 0, width, axis=dim)
        before = lax.ppermute(last, axis, up)
        after = lax.ppermute(leading, axis, down)
        x = jnp.concatenate([before, x, after], axis=dim)
    return x


def from_everyone(x, axis):
    size = lax.axis_size(axis)
    return lax.all_to_all(jnp.broadcast_to(x[None], (size, *x.shape)), axis, 0, 0, tiled=True)


def joined_along(parts, dim):
    parts = jnp.moveaxis(parts, 0, dim)
    shape = parts.shape
    return parts.reshape(*shape[:dim], shape[dim] * shape[dim + 1], *shape[dim + 2 :])


def gathered_copies(x, axis, dim):
    parts = from_everyone(x, axis)
    return joined_along(parts, dim)


def in_blocks(x, dim, size):
    before, after = (x.shape[:dim], x.shape[dim + 1 :])
    return jnp.moveaxis(x.reshape(*before, size, -1, *after), dim, 0)


def sent_and_summed(x, axis, dim):
    size = lax.axis_size(axis)
    parts = lax.all_to_all(in_blocks(x, dim, size), axis, 0, 0, tiled=True)
    return jnp.sum(parts, axis=0)


def from_behind(value, axis, steps):
    count = lax.axis_size(axis)
    leading, last = (max(0, -steps), min(count, count - steps))
    return lax.ppermute(value, axis, [(source, source + steps) for source in range(leading, last)])


def pack_rows(position, shape, corr, dest, cell, sub_count):
    owner = dest // sub_count
    row = owner * BAND + cell // NCOL
    column = cell % NCOL
    axis_x = shape[0]
    axis_y = shape[1]
    return jnp.stack(
        [
            position[0],
            position[1],
            axis_x * axis_x,
            axis_y * axis_y,
            corr * axis_x * axis_y,
            row.astype(jnp.float32) + row_offset,
            column.astype(jnp.float32),
        ]
    )


def empty_rows(width, code):
    base = jnp.zeros((7, width), jnp.float32)
    return base.at[2:4].set(1.0).at[5].set(code)


def pair_terms(gaia, wise):
    row_gap = gaia[5][:, None] - wise[5][None, :]
    col_gap = jnp.mod(gaia[6][:, None] - wise[6][None, :] + 1.0, NCOL) - 1.0
    near = (jnp.abs(row_gap) <= 1.0) & (jnp.abs(col_gap) <= 1.0)
    step_x = col_gap + gaia[0][:, None] - wise[0][None, :]
    step_y = row_gap + gaia[1][:, None] - wise[1][None, :]
    spread_x = gaia[2][:, None] + wise[2][None, :]
    spread_y = gaia[3][:, None] + wise[3][None, :]
    spread_xy = gaia[4][:, None] + wise[4][None, :]
    determinant = spread_x * spread_y - spread_xy * spread_xy
    chi_square = (
        spread_y * step_x * step_x - 2.0 * spread_xy * step_x * step_y + spread_x * step_y * step_y
    ) / determinant
    like = jnp.where(near, jnp.exp(-0.5 * chi_square) * inv_two_pi / jnp.sqrt(determinant), 0.0)
    return (
        jnp.sum(like, axis=1),
        jnp.sum(like * step_x, axis=1),
        jnp.sum(like * step_y, axis=1),
        jnp.sum(like, axis=0),
    )


def slots_of(dest, capacity):
    order = jnp.arange(dest.shape[0], dtype=jnp.int32)
    same = (dest[:, None] == dest[None, :]) & (order[None, :] < order[:, None])
    rank = jnp.sum(same.astype(jnp.int32), axis=1, dtype=jnp.int32)
    return dest * capacity + rank


def fold_columns(rows, block_width, carry, piece):
    row_totals, column_totals = carry
    count = piece.shape[1]
    blocks = piece.reshape(7, count // block_width, block_width).transpose(1, 0, 2)

    def column_step(totals, part):
        like, moment_x, moment_y, column_sums = pair_terms(rows, part)
        return (totals + jnp.stack([like, moment_x, moment_y]), column_sums)

    row_totals, column_sums = lax.scan(column_step, row_totals, blocks)
    column_totals = column_sums.reshape(-1)
    return (row_totals, column_totals)


def shards(
    gaia_pos,
    gaia_shape,
    gaia_corr,
    gaia_dest,
    gaia_cell,
    wise_pos,
    wise_shape,
    wise_corr,
    wise_dest,
    wise_cell,
):
    pix_count = lax.axis_size("pix")
    sub_count = lax.axis_size("sub")
    targets = pix_count * sub_count
    capacity = max(2, 5 * SRC_DEV // (2 * targets))
    received = targets * capacity
    block_width = received // 2
    gaia_rows = pack_rows(gaia_pos, gaia_shape, gaia_corr, gaia_dest[:, 0], gaia_cell, sub_count)
    wise_rows = pack_rows(wise_pos, wise_shape, wise_corr, wise_dest[:, 0], wise_cell, sub_count)
    gaia_slot = slots_of(gaia_dest[:, 0], capacity)
    wise_slot = slots_of(wise_dest[:, 0], capacity)
    gaia_send = empty_rows(received, empty_gaia).at[:, gaia_slot].set(gaia_rows)
    wise_send = empty_rows(received, empty_wise).at[:, wise_slot].set(wise_rows)
    gaia_here, wise_here = side_by_side((gaia_send, wise_send), ("pix", "sub"), 1, 1, 0)
    nearby = with_halo(wise_here, (("pix", 1),), received)
    members = sub_count * lax.axis_size("rep")
    start_totals = (
        jnp.zeros((3, received), jnp.float32),
        jnp.zeros((members * 3 * received,), jnp.float32),
    )
    gaia_result, column_totals = fold_columns(
        gaia_here, block_width, start_totals, gathered_copies(nearby, ("sub", "rep"), 1)
    )
    wise_part = sent_and_summed(column_totals, ("sub", "rep"), 0)
    from_upper = from_behind(wise_part[:received], "pix", -1)
    from_lower = from_behind(wise_part[2 * received :], "pix", 1)
    wise_result = wise_part[received : 2 * received] + from_lower + from_upper
    results = jnp.concatenate([gaia_result, wise_result[None, :]], axis=0)
    returned = lax.all_to_all(results, ("pix", "sub"), split_axis=1, concat_axis=1, tiled=True)
    return (returned[0][gaia_slot], returned[1:3][:, gaia_slot], returned[3][wise_slot])


def solution(mesh):
    return jax.shard_map(
        shards,
        mesh=mesh,
        in_specs=(
            P(None, ("groups", "pix", "sub", "rep")),
            P(None, ("groups", "pix", "sub", "rep")),
            P(("groups", "pix", "sub", "rep")),
            P(("groups", "pix", "sub", "rep"), None),
            P(("groups", "pix", "sub", "rep")),
            P(None, ("groups", "pix", "sub", "rep")),
            P(None, ("groups", "pix", "sub", "rep")),
            P(("groups", "pix", "sub", "rep")),
            P(("groups", "pix", "sub", "rep"), None),
            P(("groups", "pix", "sub", "rep")),
        ),
        out_specs=(
            P(("groups", "pix", "sub", "rep")),
            P(None, ("groups", "pix", "sub", "rep")),
            P(("groups", "pix", "sub", "rep")),
        ),
        check_vma=False,
    )
```

profile of v0, /device:TPU:46, one launch (start us, length us, event | category | flops | bytes accessed | tf_op | source)
XLA Modules:
  0.0 202.2 jit_solution(5425317804277985309)
XLA Ops:
  1.5 0.7 copy-done.2
  2.2 0.6 copy-done.8
  3.5 0.7 copy-done.4
  5.4 1.0 scatter_fusion.1
  6.4 1.0 scatter_fusion
  7.4 80.5 %all_to_all.29 = f32[14,128,2]{0,2,1:T(2,128)S(1)} all-to-all(f32[14,128,2]{0,2,1:T(2,128)S(1)} %bitcast.106), channel_id=1, replica_groups=mesh['groups'=2,'pix'=32,'sub'=4,'rep'=2] {'pix','sub'}, dimensions={1} | all-to-all | bytes 28672 | tf_op jit(solution)/shard_map/all_to_all | solution.py:23
  88.2 1.3 collective-permute-start.1
  89.5 4.6 %collective-permute-start = (f32[7,256]{0,1:T(8,128)S(1)}, f32[7,256]{0,1:T(8,128)S(1)}, u32[]{:S(2)}, u32[]{:S(2)}) collective-permute-start(f32[7,256]{0,1:T(8,128)S(1)} %bitcast.109), channel_id=1, source_target_pairs={{0,8},{8,16},{16,24},{24,32},{32,40},{40,48},{48,56},{56,64},{64,7... | collective-permute-start | bytes 21512 | tf_op jit(solution)/shard_map/ppermute | solution.py:37
  94.1 0.9 collective-permute-done.1
  95.1 1.5 collective-permute-done
  96.7 0.7 broadcast_in_dim.16
  97.4 4.5 %all-to-all-start.1 = ((f32[8,7,768]{2,1,0:T(8,128)}), f32[8,7,768]{2,1,0:T(8,128)S(1)}, u32[]{:S(2)}, u32[]{:S(2)}) async-start(f32[8,7,768]{2,1,0:T(8,128)} %broadcast_in_dim.16), calls=%async_computation.1 | async-start | bytes 393216 | tf_op jit(solution)/shard_map/all_to_all | solution.py:45
  102.0 4.7 %all-to-all-done.1 = f32[8,7,768]{2,1,0:T(8,128)S(1)} async-done(((f32[8,7,768]{2,1,0:T(8,128)}), f32[8,7,768]{2,1,0:T(8,128)S(1)}, u32[]{:S(2)}, u32[]{:S(2)}) %all-to-all-start.1) | async-done | bytes 172064 | tf_op jit(solution)/shard_map/all_to_all | solution.py:45
  106.6 29.2 %while.19 = (s32[]{:T(128)}, f32[3,256]{1,0:T(4,128)S(1)}, f32[48,128]{1,0:T(8,128)S(1)}, f32[7,256]{1,0:T(8,128)S(1)}, f32[48,7,128]{2,1,0:T(8,128)S(1)}, /*index=5*/s32[]{:T(128)}, s32[]{:T(128)}) while((s32[]{:T(128)}, f32[3,256]{1,0:T(4,128)S(1)}, f32[48,128]{1,0:T(8,128)S(1)}, f32[7,256]{1,0:T(8,128)S(1)}, ...), condition=%wide.region_9.10_spmd.clone, body=%wide.region_4.0_spmd.clone.sunk | while | flops 1476739 | bytes 53351 | solution.py:138
  135.8 7.8 %all_to_all.30 = f32[8,1,768]{2,1,0:T(1,128)S(1)} all-to-all(f32[8,1,768]{2,1,0:T(1,128)S(1)} %bitcast.124), channel_id=1, replica_groups=mesh['groups'=2,'pix'=32,'sub'=4,'rep'=2] {'sub','rep'}, dimensions={0} | all-to-all | bytes 49152 | tf_op jit(solution)/shard_map/all_to_all | solution.py:66
  143.7 1.3 collective-permute-start.3
  145.0 5.0 %collective-permute-start.2 = (f32[256]{0:T(256)S(1)}, f32[256]{0:T(256)S(1)}, u32[]{:S(2)}, u32[]{:S(2)}) collective-permute-start(f32[256]{0:T(256)S(1)} %get-tuple-element.202), channel_id=1, source_target_pairs={{0,8},{8,16},{16,24},{24,32},{32,40},{40,48},{48,56},{56,64},{64,7... | collective-permute-start | bytes 3080 | tf_op jit(solution)/shard_map/ppermute | solution.py:73
  150.2 1.1 collective-permute-done.2
  151.5 1.5 copy.55
  153.0 14.9 %all-to-all-start.3 = ((f32[4,128,2]{0,2,1:T(2,128)}), f32[4,128,2]{0,2,1:T(2,128)S(1)}, u32[]{:S(2)}, u32[]{:S(2)}) async-start(f32[4,128,2]{0,2,1:T(2,128)} %copy.55), calls=%async_computation.3 | async-start | bytes 262144 | tf_op jit(solution)/shard_map/all_to_all | solution.py:182
  167.9 28.5 %all-to-all-done.3 = f32[4,128,2]{0,2,1:T(2,128)S(1)} async-done(((f32[4,128,2]{0,2,1:T(2,128)}), f32[4,128,2]{0,2,1:T(2,128)S(1)}, u32[]{:S(2)}, u32[]{:S(2)}) %all-to-all-start.3) | async-done | bytes 4128 | tf_op jit(solution)/shard_map/all_to_all | solution.py:182
  197.1 1.8 gather_fusion
  199.0 0.6 gather_fusion.1
  200.5 1.8 gather_fusion.2
  (346 shorter events, 32.5 us)
Async XLA Ops:
  0.6 0.7 copy-start.6
  1.5 0.7 copy-start.2
  2.1 0.7 copy-start.8
  2.8 0.7 copy-start.7
  3.5 0.7 copy-start.4
  4.3 0.7 copy-start.9
  4.3 0.8 copy-start.3
  4.3 0.8 copy-start.11
  4.3 0.9 copy-start.10
  4.3 0.9 copy-start.5
  4.4 1.0 copy-start
  4.4 2.0 copy-start.1
  88.2 6.9 %collective-permute-start.1 = (f32[7,256]{0,1:T(8,128)S(1)}, f32[7,256]{0,1:T(8,128)S(1)}, u32[]{:S(2)}, u32[]{:S(2)}) collective-permute-start(f32[7,256]{0,1:T(8,128)S(1)} %bitcast.108), channel_id=1, source_target_pairs={{8,0},{16,8},{24,16},{32,24},{40,32},{48,40},{56,48},{64,56},{72,6... | collective-permute-start | bytes 21512 | tf_op jit(solution)/shard_map/ppermute | solution.py:38
  89.5 7.1 %collective-permute-start = (f32[7,256]{0,1:T(8,128)S(1)}, f32[7,256]{0,1:T(8,128)S(1)}, u32[]{:S(2)}, u32[]{:S(2)}) collective-permute-start(f32[7,256]{0,1:T(8,128)S(1)} %bitcast.109), channel_id=1, source_target_pairs={{0,8},{8,16},{16,24},{24,32},{32,40},{40,48},{48,56},{56,64},{64,7... | collective-permute-start | bytes 21512 | tf_op jit(solution)/shard_map/ppermute | solution.py:37
  97.4 9.3 %all-to-all-start.1 = ((f32[8,7,768]{2,1,0:T(8,128)}), f32[8,7,768]{2,1,0:T(8,128)S(1)}, u32[]{:S(2)}, u32[]{:S(2)}) async-start(f32[8,7,768]{2,1,0:T(8,128)} %broadcast_in_dim.16), calls=%async_computation.1 | async-start | bytes 393216 | tf_op jit(solution)/shard_map/all_to_all | solution.py:45
  143.7 6.5 %collective-permute-start.3 = (f32[256]{0:T(256)S(1)}, f32[256]{0:T(256)S(1)}, u32[]{:S(2)}, u32[]{:S(2)}) collective-permute-start(f32[256]{0:T(256)S(1)} %get-tuple-element.203), channel_id=1, source_target_pairs={{8,0},{16,8},{24,16},{32,24},{40,32},{48,40},{56,48},{64,56},{72,6... | collective-permute-start | bytes 3080 | tf_op jit(solution)/shard_map/ppermute | solution.py:73
  145.0 6.3 %collective-permute-start.2 = (f32[256]{0:T(256)S(1)}, f32[256]{0:T(256)S(1)}, u32[]{:S(2)}, u32[]{:S(2)}) collective-permute-start(f32[256]{0:T(256)S(1)} %get-tuple-element.202), channel_id=1, source_target_pairs={{0,8},{8,16},{16,24},{24,32},{32,40},{40,48},{48,56},{56,64},{64,7... | collective-permute-start | bytes 3080 | tf_op jit(solution)/shard_map/ppermute | solution.py:73
  153.0 43.4 %all-to-all-start.3 = ((f32[4,128,2]{0,2,1:T(2,128)}), f32[4,128,2]{0,2,1:T(2,128)S(1)}, u32[]{:S(2)}, u32[]{:S(2)}) async-start(f32[4,128,2]{0,2,1:T(2,128)} %copy.55), calls=%async_computation.3 | async-start | bytes 262144 | tf_op jit(solution)/shard_map/all_to_all | solution.py:182
where the time goes:
time: 203 us; the launch traced here: 202 us
  blocking collectives  88.3 us (43%)
  waiting for transfers between devices  36.6 us (18%)
  starting transfers between devices  31.7 us (16%)
  other arithmetic  25 us (12%)
  local copies, waits for them, and re-layouts  17.8 us (9%)
    all_to_all x1, blocking collectives, side_by_side(): lax.all_to_all(both, axis, split_axis=split_dim, concat_axis=concat_dim,...  80.5 us
    all_to_all x1, waiting for transfers between devices, shards(): lax.all_to_all(results, ('pix', 'sub'), split_axis=1, concat_axis=1, tile...  28.5 us
    reduce_sum x48, other arithmetic, pair_terms(): jnp.sum(like, axis=0)  23.5 us
    all_to_all x1, starting transfers between devices, shards(): lax.all_to_all(results, ('pix', 'sub'), split_axis=1, concat_axis=1, tile...  14.9 us
    all_to_all x1, blocking collectives, sent_and_summed(): parts = lax.all_to_all(in_blocks(x, dim, size), axis, 0, 0, tiled=True)  7.79 us
    ppermute x2, starting transfers between devices, from_behind(): lax.ppermute(value, axis, [(source, source + steps) for source in range(l...  6.33 us
    all_to_all x1, waiting for transfers between devices, from_everyone(): lax.all_to_all(jnp.broadcast_to(x[None], (size, *x.shape)), axis, 0, 0, t...  4.66 us
    unnamed x26, local copies, waits for them, and re-layouts  4.61 us
  transfers between devices with their start and end apart: 6, of which 5 were waited for; matrix products, arithmetic and copies ran while one was open for 0% of the time, Pallas kernels for 0%

commit v1 on v0

--- a/solution.py
+++ b/solution.py
@@ -179,7 +179,15 @@
     from_lower = from_behind(wise_part[2 * received :], "pix", 1)
     wise_result = wise_part[received : 2 * received] + from_lower + from_upper
     results = jnp.concatenate([gaia_result, wise_result[None, :]], axis=0)
-    returned = lax.all_to_all(results, ("pix", "sub"), split_axis=1, concat_axis=1, tiled=True)
+    returned = jnp.concatenate(
+        lax.all_to_all(
+            jnp.stack(jnp.split(results, lax.axis_size(("pix", "sub")), axis=1)),
+            ("pix", "sub"),
+            0,
+            0,
+        ),
+        axis=1,
+    )
     return (returned[0][gaia_slot], returned[1:3][:, gaia_slot], returned[3][wise_slot])
 
 

time: 203 us -> 288 us (1.42)
  local copies, waits for them, and re-layouts: 17.8 us -> 101 us
    unnamed x26 -> x153, local copies, waits for them, and re-layouts: 4.61 us -> 77.2 us
    split x0 -> x128, local copies, waits for them, and re-layouts: none -> 11.8 us  [shards(): jnp.split(results, lax.axis_size(('pix', 'sub')), axis=1)]
where the time goes in v1:
time: 288 us; the launch traced here: 287 us
  local copies, waits for them, and re-layouts  101 us (35%)
  blocking collectives  88.3 us (31%)
  waiting for transfers between devices  36.8 us (13%)
  starting transfers between devices  31.7 us (11%)
  other arithmetic  26.8 us (9%)
    all_to_all x1, blocking collectives, side_by_side(): lax.all_to_all(both, axis, split_axis=split_dim, concat_axis=concat_dim,...  80.5 us
    unnamed x153, local copies, waits for them, and re-layouts  77.2 us
    all_to_all x1, waiting for transfers between devices, shards(): lax.all_to_all(jnp.stack(jnp.split(results, lax.axis_size(('pix', 'sub'))...  28.5 us
    reduce_sum x48, other arithmetic, pair_terms(): jnp.sum(like, axis=0)  23.5 us
    all_to_all x1, starting transfers between devices, shards(): lax.all_to_all(jnp.stack(jnp.split(results, lax.axis_size(('pix', 'sub'))...  14.9 us
    split x128, local copies, waits for them, and re-layouts, shards(): jnp.split(results, lax.axis_size(('pix', 'sub')), axis=1)  11.8 us
    all_to_all x1, blocking collectives, sent_and_summed(): parts = lax.all_to_all(in_blocks(x, dim, size), axis, 0, 0, tiled=True)  7.79 us
    ppermute x2, starting transfers between devices, from_behind(): lax.ppermute(value, axis, [(source, source + steps) for source in range(l...  6.33 us
  transfers between devices with their start and end apart: 6, of which 5 were waited for; matrix products, arithmetic and copies ran while one was open for 0% of the time, Pallas kernels for 0%

profile of v1, /device:TPU:46, one launch (start us, length us, event | category | flops | bytes accessed | tf_op | source)
XLA Modules:
  0.0 287.5 jit_solution(9062337111920642723)
XLA Ops:
  0.6 0.6 copy-done.6
  1.5 0.7 copy-done.2
  2.2 0.6 copy-done.8
  3.5 0.7 copy-done.4
  5.4 1.0 scatter_fusion.1
  6.4 1.0 scatter_fusion
  7.4 80.5 %all_to_all.28 = f32[14,128,2]{0,2,1:T(2,128)S(1)} all-to-all(f32[14,128,2]{0,2,1:T(2,128)S(1)} %bitcast.388), channel_id=1, replica_groups=mesh['groups'=2,'pix'=32,'sub'=4,'rep'=2] {'pix','sub'}, dimensions={1} | all-to-all | bytes 28672 | tf_op jit(solution)/shard_map/all_to_all | solution.py:23
  88.2 1.3 collective-permute-start.1
  89.5 4.6 %collective-permute-start = (f32[7,256]{0,1:T(8,128)S(1)}, f32[7,256]{0,1:T(8,128)S(1)}, u32[]{:S(2)}, u32[]{:S(2)}) collective-permute-start(f32[7,256]{0,1:T(8,128)S(1)} %bitcast.391), channel_id=1, source_target_pairs={{0,8},{8,16},{16,24},{24,32},{32,40},{40,48},{48,56},{56,64},{64,7... | collective-permute-start | bytes 21512 | tf_op jit(solution)/shard_map/ppermute | solution.py:37
  94.1 0.9 collective-permute-done.1
  95.1 1.5 collective-permute-done
  96.7 0.7 broadcast_in_dim.19
  97.4 4.5 %all-to-all-start.1 = ((f32[8,7,768]{2,1,0:T(8,128)}), f32[8,7,768]{2,1,0:T(8,128)S(1)}, u32[]{:S(2)}, u32[]{:S(2)}) async-start(f32[8,7,768]{2,1,0:T(8,128)} %broadcast_in_dim.19), calls=%async_computation.1 | async-start | bytes 393216 | tf_op jit(solution)/shard_map/all_to_all | solution.py:45
  102.0 4.7 %all-to-all-done.1 = f32[8,7,768]{2,1,0:T(8,128)S(1)} async-done(((f32[8,7,768]{2,1,0:T(8,128)}), f32[8,7,768]{2,1,0:T(8,128)S(1)}, u32[]{:S(2)}, u32[]{:S(2)}) %all-to-all-start.1) | async-done | bytes 172064 | tf_op jit(solution)/shard_map/all_to_all | solution.py:45
  106.6 29.2 %while.19 = (s32[]{:T(128)}, f32[3,256]{1,0:T(4,128)S(1)}, f32[48,128]{1,0:T(8,128)S(1)}, f32[7,256]{1,0:T(8,128)S(1)}, f32[48,7,128]{2,1,0:T(8,128)S(1)}, /*index=5*/s32[]{:T(128)}, s32[]{:T(128)}) while((s32[]{:T(128)}, f32[3,256]{1,0:T(4,128)S(1)}, f32[48,128]{1,0:T(8,128)S(1)}, f32[7,256]{1,0:T(8,128)S(1)}, ...), condition=%wide.region_9.10_spmd.clone, body=%wide.region_4.0_spmd.clone.sunk | while | flops 1476739 | bytes 53351 | solution.py:138
  135.8 7.8 %all_to_all.29 = f32[8,1,768]{2,1,0:T(1,128)S(1)} all-to-all(f32[8,1,768]{2,1,0:T(1,128)S(1)} %bitcast.406), channel_id=1, replica_groups=mesh['groups'=2,'pix'=32,'sub'=4,'rep'=2] {'sub','rep'}, dimensions={0} | all-to-all | bytes 49152 | tf_op jit(solution)/shard_map/all_to_all | solution.py:66
  143.7 1.3 collective-permute-start.3
  145.0 5.0 %collective-permute-start.2 = (f32[256]{0:T(256)S(1)}, f32[256]{0:T(256)S(1)}, u32[]{:S(2)}, u32[]{:S(2)}) collective-permute-start(f32[256]{0:T(256)S(1)} %get-tuple-element.338), channel_id=1, source_target_pairs={{0,8},{8,16},{16,24},{24,32},{32,40},{40,48},{48,56},{56,64},{64,7... | collective-permute-start | bytes 3080 | tf_op jit(solution)/shard_map/ppermute | solution.py:73
  150.0 1.3 collective-permute-done.2
  238.2 14.9 %all-to-all-start.3 = ((f32[128,4,2]{1,2,0:T(2,128)}), f32[128,4,2]{1,2,0:T(2,128)S(1)}, u32[]{:S(2)}, u32[]{:S(2)}) async-start(f32[128,4,2]{1,2,0:T(2,128)} %constant_dynamic-update-slice_fusion), calls=%async_computation.3 | async-start | bytes 262144 | tf_op jit(solution)/shard_map/all_to_all | solution.py:183
  253.1 28.5 %all-to-all-done.3 = f32[128,4,2]{1,2,0:T(2,128)S(1)} async-done(((f32[128,4,2]{1,2,0:T(2,128)}), f32[128,4,2]{1,2,0:T(2,128)S(1)}, u32[]{:S(2)}, u32[]{:S(2)}) %all-to-all-start.3) | async-done | bytes 4128 | tf_op jit(solution)/shard_map/all_to_all | solution.py:183
  282.5 1.8 gather_fusion
  284.3 0.6 gather_fusion.1
  285.7 1.8 gather_fusion.2
  (619 shorter events, 118.2 us)
Async XLA Ops:
  0.6 0.7 copy-start.6
  1.5 0.7 copy-start.2
  2.1 0.7 copy-start.8
  2.8 0.7 copy-start.7
  3.5 0.7 copy-start.4
  4.3 0.7 copy-start.9
  4.3 0.8 copy-start.3
  4.3 0.8 copy-start.11
  4.3 0.9 copy-start.10
  4.3 0.9 copy-start.5
  4.4 1.0 copy-start
  4.4 2.0 copy-start.1
  88.2 6.9 %collective-permute-start.1 = (f32[7,256]{0,1:T(8,128)S(1)}, f32[7,256]{0,1:T(8,128)S(1)}, u32[]{:S(2)}, u32[]{:S(2)}) collective-permute-start(f32[7,256]{0,1:T(8,128)S(1)} %bitcast.390), channel_id=1, source_target_pairs={{8,0},{16,8},{24,16},{32,24},{40,32},{48,40},{56,48},{64,56},{72,6... | collective-permute-start | bytes 21512 | tf_op jit(solution)/shard_map/ppermute | solution.py:38
  89.5 7.1 %collective-permute-start = (f32[7,256]{0,1:T(8,128)S(1)}, f32[7,256]{0,1:T(8,128)S(1)}, u32[]{:S(2)}, u32[]{:S(2)}) collective-permute-start(f32[7,256]{0,1:T(8,128)S(1)} %bitcast.391), channel_id=1, source_target_pairs={{0,8},{8,16},{16,24},{24,32},{32,40},{40,48},{48,56},{56,64},{64,7... | collective-permute-start | bytes 21512 | tf_op jit(solution)/shard_map/ppermute | solution.py:37
  97.4 9.3 %all-to-all-start.1 = ((f32[8,7,768]{2,1,0:T(8,128)}), f32[8,7,768]{2,1,0:T(8,128)S(1)}, u32[]{:S(2)}, u32[]{:S(2)}) async-start(f32[8,7,768]{2,1,0:T(8,128)} %broadcast_in_dim.19), calls=%async_computation.1 | async-start | bytes 393216 | tf_op jit(solution)/shard_map/all_to_all | solution.py:45
  143.7 6.4 %collective-permute-start.3 = (f32[256]{0:T(256)S(1)}, f32[256]{0:T(256)S(1)}, u32[]{:S(2)}, u32[]{:S(2)}) collective-permute-start(f32[256]{0:T(256)S(1)} %get-tuple-element.339), channel_id=1, source_target_pairs={{8,0},{16,8},{24,16},{32,24},{40,32},{48,40},{56,48},{64,56},{72,6... | collective-permute-start | bytes 3080 | tf_op jit(solution)/shard_map/ppermute | solution.py:73
  145.0 6.3 %collective-permute-start.2 = (f32[256]{0:T(256)S(1)}, f32[256]{0:T(256)S(1)}, u32[]{:S(2)}, u32[]{:S(2)}) collective-permute-start(f32[256]{0:T(256)S(1)} %get-tuple-element.338), channel_id=1, source_target_pairs={{0,8},{8,16},{16,24},{24,32},{32,40},{40,48},{48,56},{56,64},{64,7... | collective-permute-start | bytes 3080 | tf_op jit(solution)/shard_map/ppermute | solution.py:73
  238.2 43.4 %all-to-all-start.3 = ((f32[128,4,2]{1,2,0:T(2,128)}), f32[128,4,2]{1,2,0:T(2,128)S(1)}, u32[]{:S(2)}, u32[]{:S(2)}) async-start(f32[128,4,2]{1,2,0:T(2,128)} %constant_dynamic-update-slice_fusion), calls=%async_computation.3 | async-start | bytes 262144 | tf_op jit(solution)/shard_map/all_to_all | solution.py:183
